TPU v7x, 32 devices: a whole 2x2x4 slice. The times are simulated.
32 devices in a mesh: dp: 8 (over z, x), expert: 4 (over y, core).
Axes of the slice: x: 2, y: 2, z: 4, core: 2. Of those that a mesh axis runs over, the one named last changes fastest.
Arguments:
- tokens: bfloat16 [4096, 4096], P(('dp', 'expert')), may hold values from -6 to 6
- grad_out: bfloat16 [4096, 4096], P(('dp', 'expert')), may hold values from -6 to 6
- experts: int32 [4096, 2], P(('dp', 'expert')), may hold values from 0 to 7, all different within a row; in each aligned block of 128 rows (0 to 127, 128 to 255, ...) at most 64 rows name the same one
- gates: bfloat16 [4096, 2], P(('dp', 'expert')), may hold values from 0 to 1, as said below
- router_weight: bfloat16 [8, 4096], replicated, may hold values from -3 to 3
- saved_outputs: bfloat16 [16384, 4096], P(('dp', 'expert')), may hold values from -0.19921875 to 0.19921875
Outputs:
- input_grad: bfloat16 [4096, 4096], P(('dp', 'expert'))
- router_grad: float32 [8, 4096], replicated
- expert_grad: bfloat16 [16384, 4096], P(('dp', 'expert'))
Inputs may be any that keep to these rules, and one draw needn't show every extreme that they name: Within each aligned block of 128 tokens (the tokens of one device), no expert is named by more than 64 slots, and in some blocks an expert is named by exactly 64 slots. The two experts of a token differ. The two gates of a token are positive and add up to one, up to rounding to bfloat16.
All inputs are finite; a program needn't handle non-finite values.
Results may differ from a plain program's by a relative error of at most 0.0085.
Values may be sent and summed in bfloat16 or wider, within the bound.
A program may use at most 64 MiB of HBM per device.

v0:
```python
import jax
import jax.numpy as jnp
from jax import lax
from jax.sharding import PartitionSpec as P


def slot_positions(experts, count):
    slot_expert = experts.reshape(-1)
    onehot = (slot_expert[:, None] == jnp.arange(count, dtype=jnp.int32)[None, :]).astype(jnp.int32)
    before = jnp.cumsum(onehot, axis=0) - onehot
    return (slot_expert, jnp.sum(before * onehot, axis=1))


def local(tokens, grad_out, experts, gates, router_weight, saved_outputs):
    groups = lax.axis_size("expert")
    chosen_count = experts.shape[1]
    expert_count = router_weight.shape[0]
    held = expert_count // groups
    capacity = tokens.shape[0] // 2
    width = saved_outputs.shape[1]
    slot_expert, position = slot_positions(experts, expert_count)
    target = slot_expert % held * (groups * capacity) + slot_expert // held * capacity + position
    slot_gates = gates.reshape(-1)
    repeated = jnp.repeat(grad_out, chosen_count, axis=0)
    layout = (held, groups * capacity, width)
    returned = lax.all_to_all(
        saved_outputs.reshape(layout), "expert", split_axis=1, concat_axis=1, tiled=True
    )
    picked = returned.reshape(-1, width)[target]
    products = jnp.einsum("sd,sd->s", repeated, picked, preferred_element_type=jnp.float32)
    weighted = (slot_gates.astype(jnp.float32)[:, None] * repeated.astype(jnp.float32)).astype(
        jnp.bfloat16
    )
    buffer = jnp.zeros(saved_outputs.shape, jnp.bfloat16).at[target].set(weighted)
    expert_grad = lax.all_to_all(
        buffer.reshape(layout), "expert", split_axis=1, concat_axis=1, tiled=True
    ).reshape(-1, width)
    gate_grad = products.reshape(-1, chosen_count)
    gate_values = gates.astype(jnp.float32)
    blended = jnp.sum(gate_values * gate_grad, axis=1, keepdims=True)
    slot_grad = gate_values * (gate_grad - blended)
    onehot = (
        experts[:, :, None] == jnp.arange(expert_count, dtype=jnp.int32)[None, None, :]
    ).astype(jnp.float32)
    logit_grad = jnp.sum(onehot * slot_grad[:, :, None], axis=1).astype(jnp.bfloat16)
    partial_value = lax.dot_general(
        logit_grad, tokens, (((0,), (0,)), ((), ())), preferred_element_type=jnp.float32
    )
    summed = lax.psum(partial_value, ("dp", "expert"))
    scale_factor = float(lax.axis_size("dp") * groups * tokens.shape[0]) ** (-0.5)
    router_grad = summed * scale_factor
    input_grad = jnp.dot(logit_grad, router_weight, preferred_element_type=jnp.float32).astype(
        jnp.bfloat16
    )
    return (input_grad, router_grad, expert_grad)


def solution(mesh):
    return jax.shard_map(
        local,
        mesh=mesh,
        in_specs=(
            P(("dp", "expert"), None),
            P(("dp", "expert"), None),
            P(("dp", "expert"), None),
            P(("dp", "expert"), None),
            P(),
            P(("dp", "expert"), None),
        ),
        out_specs=(P(("dp", "expert"), None), P(), P(("dp", "expert"), None)),
        check_vma=False,
    )
```

profile of v0, /device:TPU:0, one launch (start us, length us, event | category | flops | bytes accessed | tf_op | source)
XLA Modules:
  0.0 228.8 jit_solution(14404547339752662202)
XLA Ops:
  7.2 0.0 copy-start
  7.2 8.7 %copy.40 = bf16[2,256,4096]{2,0,1:T(2,128)(2,1)} copy(bf16[2,256,4096]{2,1,0:T(8,128)(2,1)} %bitcast.20) | data formatting | bytes 8388608 | tf_op jit(solution)/shard_map/reshape | solution.py:27
  15.9 0.0 copy-start.4
  15.9 0.0 copy-start.1
  15.9 5.0 %all-to-all-start = ((bf16[2,256,4096]{2,0,1:T(2,128)(2,1)}), bf16[2,256,4096]{2,0,1:T(2,128)(2,1)}, u32[]{:S(2)}, u32[]{:S(2)}) async-start(bf16[2,256,4096]{2,0,1:T(2,128)(2,1)} %copy.40), calls=%async_computation | async-start | bytes 8388608 | tf_op jit(solution)/shard_map/all_to_all | solution.py:26
  20.9 0.0 copy-done.4
  20.9 0.0 copy-start.3
  20.9 0.1 copy.42
  21.0 0.1 eq.47
  21.2 0.1 eq.43
  21.3 0.1 reshape.177
  21.4 0.6 reduce-window.6
  22.0 0.2 slice_reduce_fusion
  22.3 0.0 copy-done.1
  22.3 3.5 %broadcast_in_dim.4 = bf16[128,2,4096]{2,1,0:T(2,128)(2,1)} broadcast(bf16[128,4096]{1,0:T(8,128)(2,1)S(1)} %copy-done.1), dimensions={0,2} | broadcast | bytes 3145728 | tf_op jit(solution)/shard_map/broadcast_in_dim | solution.py:24
  25.8 2.7 %reshape.179 = bf16[256,4096]{1,0:T(8,128)(2,1)S(1)} reshape(bf16[128,2,4096]{2,1,0:T(2,128)(2,1)} %broadcast_in_dim.4) | data formatting | bytes 4194304 | tf_op jit(solution)/shard_map/reshape | solution.py:24
  28.5 0.0 copy-done.3
  28.5 0.1 copy.47
  28.6 0.1 reshape.183
  28.8 0.1 fusion.7
  28.9 6.1 %scatter_custom_fusion = bf16[512,4096]{1,0:T(8,128)(2,1)} fusion(s32[256]{0:T(256)S(1)} %bitcast.22, bf16[256,4096]{1,0:T(8,128)(2,1)S(1)} %reshape.179, f32[256]{0:T(256)S(1)} %reshape.183, bf16[]{:T(256)} %constant.44.clone.1), kind=kCustom, calls=%fused_computation.7 | custom fusion | flops 3145728 | bytes 6292482 | tf_op jit(solution)/shard_map/scatter | solution.py:34
  35.0 8.6 %copy.48 = bf16[2,256,4096]{2,0,1:T(2,128)(2,1)} copy(bf16[2,256,4096]{2,1,0:T(8,128)(2,1)} %bitcast.19) | data formatting | bytes 8388608 | tf_op jit(solution)/shard_map/reshape | solution.py:36
  43.6 26.2 %all-to-all-done = bf16[2,256,4096]{2,0,1:T(2,128)(2,1)} async-done(((bf16[2,256,4096]{2,0,1:T(2,128)(2,1)}), bf16[2,256,4096]{2,0,1:T(2,128)(2,1)}, u32[]{:S(2)}, u32[]{:S(2)}) %all-to-all-start) | async-done | bytes 4194336 | tf_op jit(solution)/shard_map/all_to_all | solution.py:26
  69.8 4.9 %all-to-all-start.1 = ((bf16[2,256,4096]{2,0,1:T(2,128)(2,1)}), bf16[2,256,4096]{2,0,1:T(2,128)(2,1)}, u32[]{:S(2)}, u32[]{:S(2)}) async-start(bf16[2,256,4096]{2,0,1:T(2,128)(2,1)} %copy.48), calls=%async_computation.1 | async-start | bytes 8388608 | tf_op jit(solution)/shard_map/all_to_all | solution.py:35
  74.7 0.0 all-reduce.2.cloned.1.call-start
  74.8 7.1 %copy.41 = bf16[2,256,4096]{2,1,0:T(8,128)(2,1)} copy(bf16[2,256,4096]{2,0,1:T(2,128)(2,1)} %all-to-all-done) | data formatting | bytes 8388608 | tf_op jit(solution)/shard_map/all_to_all | solution.py:26
  81.9 8.0 %gather_fusion = bf16[256,4096]{1,0:T(8,128)(2,1)} fusion(bf16[512,4096]{1,0:T(8,128)(2,1)} %bitcast.18, s32[1024]{0:T(1024)S(1)} %pad_clamp_fusion), kind=kCustom, calls=%fused_computation | custom fusion | bytes 4195328 | tf_op jit(solution)/shard_map/gather | solution.py:29
  89.8 0.0 copy-start.2
  89.8 2.2 fusion
  92.1 0.1 reshape.180
  92.2 0.1 copy.46
  92.4 0.0 copy-done
  92.4 0.9 fusion.15
  93.3 0.0 all-reduce.2.cloned.1.call-update
  93.3 0.0 copy-done.2
  93.3 1.4 convolution_convert_fusion
  94.8 28.4 %all-to-all-done.1 = bf16[2,256,4096]{2,0,1:T(2,128)(2,1)} async-done(((bf16[2,256,4096]{2,0,1:T(2,128)(2,1)}), bf16[2,256,4096]{2,0,1:T(2,128)(2,1)}, u32[]{:S(2)}, u32[]{:S(2)}) %all-to-all-start.1) | async-done | bytes 4194336 | tf_op jit(solution)/shard_map/all_to_all | solution.py:35
  123.2 7.1 %copy.49 = bf16[2,256,4096]{2,1,0:T(8,128)(2,1)} copy(bf16[2,256,4096]{2,0,1:T(2,128)(2,1)} %all-to-all-done.1) | data formatting | bytes 8388608 | tf_op jit(solution)/shard_map/all_to_all | solution.py:35
  130.3 90.1 %all-reduce.2.cloned.1.call-done = f32[8,4096]{1,0:T(8,128)} async-done(((f32[8,4096]{1,0:T(8,128)}), f32[8,4096]{1,0:T(8,128)}) %all-reduce.2.cloned.1.call-update) | async-done | bytes 131088 | tf_op jit(solution)/shard_map/psum | solution.py:49
  220.4 1.6 broadcast_multiply_fusion
  (8 shorter events, 0.1 us)
Async XLA Ops:
  7.2 85.2 %copy-start = (bf16[128,4096]{1,0:T(8,128)(2,1)S(1)}, bf16[128,4096]{1,0:T(8,128)(2,1)}, u32[]{:S(2)}) copy-start(bf16[128,4096]{1,0:T(8,128)(2,1)} %param.6) | copy-start | bytes 3145732
  15.9 5.0 %copy-start.4 = (s32[128,2]{0,1:T(2,128)S(1)}, s32[128,2]{0,1:T(2,128)}, u32[]{:S(2)}) copy-start(s32[128,2]{0,1:T(2,128)} %param.8) | copy-start | bytes 3076
  15.9 6.4 %copy-start.1 = (bf16[128,4096]{1,0:T(8,128)(2,1)S(1)}, bf16[128,4096]{1,0:T(8,128)(2,1)}, u32[]{:S(2)}) copy-start(bf16[128,4096]{1,0:T(8,128)(2,1)} %param.7) | copy-start | bytes 3145732
  15.9 53.9 %all-to-all-start = ((bf16[2,256,4096]{2,0,1:T(2,128)(2,1)}), bf16[2,256,4096]{2,0,1:T(2,128)(2,1)}, u32[]{:S(2)}, u32[]{:S(2)}) async-start(bf16[2,256,4096]{2,0,1:T(2,128)(2,1)} %copy.40), calls=%async_computation | async-start | bytes 8388608 | tf_op jit(solution)/shard_map/all_to_all | solution.py:26
  20.9 7.6 %copy-start.3 = (bf16[128,2]{0,1:T(2,128)(2,1)S(1)}, bf16[128,2]{0,1:T(2,128)(2,1)}, u32[]{:S(2)}) copy-start(bf16[128,2]{0,1:T(2,128)(2,1)} %param.9) | copy-start | bytes 1540
  69.8 53.4 %all-to-all-start.1 = ((bf16[2,256,4096]{2,0,1:T(2,128)(2,1)}), bf16[2,256,4096]{2,0,1:T(2,128)(2,1)}, u32[]{:S(2)}, u32[]{:S(2)}) async-start(bf16[2,256,4096]{2,0,1:T(2,128)(2,1)} %copy.48), calls=%async_computation.1 | async-start | bytes 8388608 | tf_op jit(solution)/shard_map/all_to_all | solution.py:35
  74.7 145.7 %all-reduce.2.cloned.1.call-start = ((), (), s32[]{:S(2)}) async-start(), calls=%async_computation.2 | async-start | bytes 262144 | tf_op jit(solution)/shard_map/psum | solution.py:49
  89.8 3.5 %copy-start.2 = (bf16[8,4096]{1,0:T(8,128)(2,1)S(1)}, bf16[8,4096]{1,0:T(8,128)(2,1)}, u32[]{:S(2)}) copy-start(bf16[8,4096]{1,0:T(8,128)(2,1)} %param.10) | copy-start | bytes 196612
Sparse Core Ops, SparseCore 0:
  93.4 126.8 all-reduce.1
where the time goes:
time: 229 us
  waiting for transfers between devices  145 us (63%)
  local copies, waits for them, and re-layouts  46.9 us (20%)
  between operations  14.2 us (6%)
  other arithmetic  10.7 us (5%)
  starting transfers between devices  9.97 us (4%)
  matrix products  2.36 us (1%)
    psum x1, waiting for transfers between devices, local(): summed = lax.psum(partial_value, ('dp', 'expert'))  90.1 us
    all_to_all x1, waiting for transfers between devices, local(): lax.all_to_all(buffer.reshape(layout), 'expert', split_axis=1, concat_axi...  28.4 us
    all_to_all x1, waiting for transfers between devices, local(): lax.all_to_all(saved_outputs.reshape(layout), 'expert', split_axis=1, con...  26.2 us
    reshape x1, local copies, waits for them, and re-layouts, local(): saved_outputs.reshape(layout)  8.69 us
    reshape x1, local copies, waits for them, and re-layouts, local(): buffer.reshape(layout)  8.56 us
    gather x1, local copies, waits for them, and re-layouts, local(): picked = returned.reshape(-1, width)[target]  7.96 us
    all_to_all x1, local copies, waits for them, and re-layouts, local(): lax.all_to_all(buffer.reshape(layout), 'expert', split_axis=1, concat_axi...  7.13 us
    all_to_all x1, local copies, waits for them, and re-layouts, local(): lax.all_to_all(saved_outputs.reshape(layout), 'expert', split_axis=1, con...  7.11 us
  transfers between devices with their start and end apart: 3, of which 3 were waited for; matrix products, arithmetic and copies ran while one was open for 22% of the time, Pallas kernels for 0%

commit v1 on v0

v1 whole, which is shorter than its diff:
```python
import functools

import jax
import jax.numpy as jnp
from jax import lax
from jax.experimental import pallas as pl
from jax.experimental.pallas import tpu as pltpu
from jax.sharding import PartitionSpec as P

MESH = pl.DeviceIdType.MESH
F32 = jnp.float32
BF16 = jnp.bfloat16


def exchange_kernel(
    n, m, pieces, scale,
    info_ref, g_ref, tok_ref, saved_ref,
    g_out, w_out, logit_out, router_out,
    slots, saved_v, tok_v, meta_own, meta_in, ret_own, ret_in,
    acc_a, acc_b, part, part_in, dp_in, fin, fin_in,
    g_send, g_recv, meta_send, meta_recv, ret_send, ret_recv,
    part_send, part_recv, dp_send, dp_recv, fin_send, fin_recv,
    saved_sem, tok_sem, gout_sem,
):
    held, _, cap, width = saved_ref.shape
    rows = held * cap
    tokens = g_ref.shape[0]
    experts = logit_out.shape[1]
    piece = width // pieces
    share = width // n
    pairs = n // 2
    me = lax.axis_index("expert")
    dp = lax.axis_index("dp")
    parity = me % 2
    pair = me // 2

    def source(j):
        q, flip = j // 2, j % 2
        low = parity if flip == 0 else 1 - parity
        return ((pair - q + pairs) % pairs) * 2 + low

    def target(j):
        q, flip = j // 2, j % 2
        low = parity if flip == 0 else 1 - parity
        return ((pair + q) % pairs) * 2 + low

    def cols(c):
        return pl.ds(pl.multiple_of(c * piece, piece), piece)

    barrier = pltpu.get_barrier_semaphore()
    for j in range(1, n):
        pl.semaphore_signal(barrier, inc=1, device_id={"expert": target(j)}, device_id_type=MESH)

    def greet(i, carry):
        pl.semaphore_signal(barrier, inc=1, device_id={"dp": (dp + i) % m}, device_id_type=MESH)
        return carry

    lax.fori_loop(1, m, greet, 0)

    def saved_copy(j, h):
        return pltpu.make_async_copy(
            saved_ref.at[h, source(j)],
            saved_v.at[j, pl.ds(h * cap, cap)],
            saved_sem.at[j, h],
        )

    for j in range(n):
        for h in range(held):
            saved_copy(j, h).start()
    tok_copy = pltpu.make_async_copy(tok_ref, tok_v, tok_sem)
    tok_copy.start()
    own_out = pltpu.make_async_copy(g_ref, g_out.at[me], gout_sem.at[0])
    own_out.start()

    expert_ids = lax.broadcasted_iota(jnp.int32, (experts, tokens), 0).astype(F32)
    hot = [(info_ref[k : k + 1, :] == expert_ids).astype(F32) for k in range(2)]
    earlier = (
        lax.broadcasted_iota(jnp.int32, (tokens, tokens), 0)
        < lax.broadcasted_iota(jnp.int32, (tokens, tokens), 1)
    ).astype(F32).astype(BF16)
    before = jnp.dot((hot[0] + hot[1]).astype(BF16), earlier, preferred_element_type=F32)
    meta_own[...] = info_ref[...]
    for k in range(2):
        position = jnp.sum(before * hot[k], axis=0, keepdims=True)
        meta_own[k : k + 1, :] = info_ref[k : k + 1, :] * float(cap) + position

    pl.semaphore_wait(barrier, n + m - 2)

    def g_copy(src, j, c, to):
        return pltpu.make_async_remote_copy(
            src_ref=src,
            dst_ref=slots.at[j - 1, :, cols(c)],
            send_sem=g_send.at[j - 1, c],
            recv_sem=g_recv.at[j - 1, c],
            device_id={"expert": to},
            device_id_type=MESH,
        )

    def small_copy(src, dst, send, recv, j, to):
        return pltpu.make_async_remote_copy(
            src_ref=src,
            dst_ref=dst.at[j - 1],
            send_sem=send.at[j - 1],
            recv_sem=recv.at[j - 1],
            device_id={"expert": to},
            device_id_type=MESH,
        )

    meta_copies = [
        small_copy(meta_own, meta_in, meta_send, meta_recv, j, target(j)) for j in range(1, n)
    ]
    for copy in meta_copies:
        copy.start()
    for q in range(1, pairs):

        def send_direct(c, carry, q=q):
            g_copy(g_ref.at[:, cols(c)], 2 * q, c, target(2 * q)).start()
            return carry

        lax.fori_loop(0, pieces, send_direct, 0)

    def send_partner(c, carry):
        g_copy(g_ref.at[:, cols(c)], 1, c, target(1)).start()
        return carry

    lax.fori_loop(0, pieces, send_partner, 0)

    row_ids = lax.broadcasted_iota(jnp.int32, (rows, tokens), 0).astype(F32)
    base = (me * rows).astype(F32)

    def masks(meta):
        return [meta[k : k + 1, :] - base == row_ids for k in range(2)]

    def write_weights(j, meta):
        named = masks(meta)
        weights = jnp.where(named[0], meta[2:3, :], 0.0) + jnp.where(named[1], meta[3:4, :], 0.0)
        w_out[source(j)] = weights.astype(BF16)

    def product(j, c, right):
        return lax.dot_general(
            saved_v[j, :, cols(c)], right, (((1,), (1,)), ((), ())), preferred_element_type=F32
        )

    def picked(meta, total):
        return [
            jnp.sum(jnp.where(named, total, 0.0), axis=0, keepdims=True) for named in masks(meta)
        ]

    def wait_saved(j):
        for h in range(held):
            saved_copy(j, h).wait()

    ret_copies = [
        small_copy(ret_own.at[j - 1], ret_in, ret_send, ret_recv, j, source(j))
        for j in range(1, n)
    ]

    def give_back(j, total):
        first, second = picked(meta_in[j - 1], total)
        ret_own[j - 1, 0:1, :] = first
        ret_own[j - 1, 1:2, :] = second
        ret_copies[j - 1].start()

    ret_own[...] = jnp.zeros_like(ret_own)
    wait_saved(0)
    write_weights(0, meta_own[...])
    zero = jnp.zeros((rows, tokens), F32)
    own_total = lax.fori_loop(
        0, pieces, lambda c, total: total + product(0, c, g_ref[:, cols(c)]), zero
    )
    own_first, own_second = picked(meta_own[...], own_total)

    for j in range(1, n):
        meta_copies[j - 1].wait_recv()
        write_weights(j, meta_in[j - 1])

    def arrived(j, c):
        g_copy(slots.at[j - 1, :, cols(c)], j, c, target(j)).wait_recv()

    def take(j, c, acc):
        acc[...] += product(j, c, slots[j - 1, :, cols(c)])

    outs = [own_out]

    def put_out(j):
        copy = pltpu.make_async_copy(slots.at[j - 1], g_out.at[source(j)], gout_sem.at[j])
        copy.start()
        outs.append(copy)

    acc_a[...] = zero
    wait_saved(1)

    def partner_step(c, carry):
        arrived(1, c)
        take(1, c, acc_a)
        return carry

    lax.fori_loop(0, pieces, partner_step, 0)
    put_out(1)
    give_back(1, acc_a[...])

    for q in range(1, pairs):
        direct, relayed = 2 * q, 2 * q + 1
        acc_a[...] = zero
        acc_b[...] = zero
        wait_saved(direct)
        wait_saved(relayed)

        def direct_step(c, direct=direct, relayed=relayed):
            arrived(direct, c)
            g_copy(slots.at[direct - 1, :, cols(c)], relayed, c, target(1)).start()
            take(direct, c, acc_a)

        def relayed_step(c, relayed=relayed):
            arrived(relayed, c)
            take(relayed, c, acc_b)

        direct_step(0)

        def step(c, carry, direct_step=direct_step, relayed_step=relayed_step):
            direct_step(c)
            relayed_step(c - 1)
            return carry

        lax.fori_loop(1, pieces, step, 0)
        put_out(direct)
        give_back(direct, acc_a[...])
        relayed_step(pieces - 1)
        put_out(relayed)
        give_back(relayed, acc_b[...])

    grads = [own_first, own_second]
    for j in range(1, n):
        ret_copies[j - 1].wait_recv()
        grads = [grads[k] + ret_in[j - 1, k : k + 1, :] for k in range(2)]
    gates = [info_ref[2 + k : 3 + k, :] for k in range(2)]
    blended = gates[0] * grads[0] + gates[1] * grads[1]
    logit = hot[0] * (gates[0] * (grads[0] - blended)) + hot[1] * (gates[1] * (grads[1] - blended))
    logit_low = logit.astype(BF16)
    tok_copy.wait()
    for j in range(n):
        part[j] = jnp.dot(
            logit_low, tok_v[:, j * share : (j + 1) * share], preferred_element_type=F32
        )

    part_copies = [
        small_copy(part.at[target(j)], part_in, part_send, part_recv, j, target(j))
        for j in range(1, n)
    ]
    for copy in part_copies:
        copy.start()
    logit_out[...] = logit.T.astype(BF16)
    total = part[me]
    for j in range(1, n):
        part_copies[j - 1].wait_recv()
        total = total + part_in[j - 1]
    dp_in[dp] = total

    def dp_copy(slot, i):
        return pltpu.make_async_remote_copy(
            src_ref=dp_in.at[dp],
            dst_ref=dp_in.at[slot],
            send_sem=dp_send.at[i],
            recv_sem=dp_recv.at[i],
            device_id={"dp": (dp + i) % m},
            device_id_type=MESH,
        )

    def dp_start(i, carry):
        dp_copy(dp, i).start()
        return carry

    def dp_wait(i, carry):
        dp_copy((dp - i + m) % m, i).wait_recv()
        return carry

    lax.fori_loop(1, m, dp_start, 0)
    lax.fori_loop(1, m, dp_wait, 0)
    fin[...] = (
        lax.fori_loop(0, m, lambda i, t: t + dp_in[i], jnp.zeros((experts, share), F32)) * scale
    )
    fin_copies = [small_copy(fin, fin_in, fin_send, fin_recv, j, target(j)) for j in range(1, n)]
    for copy in fin_copies:
        copy.start()

    def lanes(k):
        return pl.ds(pl.multiple_of(k * share, share), share)

    router_out[:, lanes(me)] = fin[...]

    def g_sent(c, carry):
        g_copy(g_ref.at[:, cols(c)], 1, c, target(1)).wait_send()
        for q in range(1, pairs):
            g_copy(g_ref.at[:, cols(c)], 2 * q, c, target(2 * q)).wait_send()
            g_copy(slots.at[2 * q - 1, :, cols(c)], 2 * q + 1, c, target(1)).wait_send()
        return carry

    lax.fori_loop(0, pieces, g_sent, 0)

    def dp_sent(i, carry):
        dp_copy(dp, i).wait_send()
        return carry

    lax.fori_loop(1, m, dp_sent, 0)
    for copy in meta_copies + ret_copies + part_copies + fin_copies:
        copy.wait_send()
    for copy in outs:
        copy.wait()
    for j in range(1, n):
        fin_copies[j - 1].wait_recv()
        router_out[:, lanes(source(j))] = fin_in[j - 1]


def exchange(info, grad_out, tokens, saved, experts, n, m):
    held, _, cap, width = saved.shape
    count = tokens.shape[0]
    rows = held * cap
    pieces = max(1, width // 512)
    share = width // n
    scale = float(m * n * count) ** (-0.5)
    dma = pltpu.SemaphoreType.DMA
    vmem = pl.BlockSpec(memory_space=pltpu.VMEM)
    anywhere = pl.BlockSpec(memory_space=pl.ANY)
    return pl.pallas_call(
        functools.partial(exchange_kernel, n, m, pieces, scale),
        name="exchange",
        out_shape=(
            jax.ShapeDtypeStruct((n, count, width), BF16),
            jax.ShapeDtypeStruct((n, rows, count), BF16),
            jax.ShapeDtypeStruct((count, experts), BF16),
            jax.ShapeDtypeStruct((experts, width), F32),
        ),
        in_specs=[vmem, vmem, anywhere, anywhere],
        out_specs=(anywhere, vmem, vmem, vmem),
        scratch_shapes=[
            pltpu.VMEM((n - 1, count, width), BF16),
            pltpu.VMEM((n, rows, width), BF16),
            pltpu.VMEM((count, width), BF16),
            pltpu.VMEM((8, count), F32),
            pltpu.VMEM((n - 1, 8, count), F32),
            pltpu.VMEM((n - 1, 8, count), F32),
            pltpu.VMEM((n - 1, 8, count), F32),
            pltpu.VMEM((rows, count), F32),
            pltpu.VMEM((rows, count), F32),
            pltpu.VMEM((n, experts, share), F32),
            pltpu.VMEM((n - 1, experts, share), F32),
            pltpu.VMEM((m, experts, share), F32),
            pltpu.VMEM((experts, share), F32),
            pltpu.VMEM((n - 1, experts, share), F32),
            dma((n - 1, pieces)), dma((n - 1, pieces)),
            dma((n - 1,)), dma((n - 1,)),
            dma((n - 1,)), dma((n - 1,)),
            dma((n - 1,)), dma((n - 1,)),
            dma((m,)), dma((m,)),
            dma((n - 1,)), dma((n - 1,)),
            dma((n, held)), dma, dma((n,)),
        ],
        compiler_params=pltpu.CompilerParams(
            collective_id=0, has_side_effects=True, vmem_limit_bytes=48 << 20
        ),
    )(info, grad_out, tokens, saved)


def finish_kernel(w_ref, g_ref, logit_ref, rw_ref, eg_ref, ig_ref):
    held, cap = eg_ref.shape[0], eg_ref.shape[2]
    spread = jnp.dot(w_ref[0], g_ref[0], preferred_element_type=F32).astype(BF16)
    for h in range(held):
        eg_ref[h, 0] = spread[h * cap : (h + 1) * cap]
    ig_ref[...] = jnp.dot(logit_ref[...], rw_ref[...], preferred_element_type=F32).astype(BF16)


def finish(weights, gathered, logit, router_weight, layout):
    held, n, cap, width = layout
    count, experts = logit.shape
    rows = held * cap
    split = 2
    block = width // split
    return pl.pallas_call(
        finish_kernel,
        name="finish",
        grid=(n, split),
        out_shape=(
            jax.ShapeDtypeStruct(layout, BF16),
            jax.ShapeDtypeStruct((count, width), BF16),
        ),
        in_specs=[
            pl.BlockSpec((1, rows, count), lambda s, c: (s, 0, 0)),
            pl.BlockSpec((1, count, block), lambda s, c: (s, 0, c)),
            pl.BlockSpec((count // n, experts), lambda s, c: (s, 0)),
            pl.BlockSpec((experts, block), lambda s, c: (0, c)),
        ],
        out_specs=(
            pl.BlockSpec((held, 1, cap, block), lambda s, c: (0, s, 0, c)),
            pl.BlockSpec((count // n, block), lambda s, c: (s, c)),
        ),
    )(weights, gathered, logit, router_weight)


def local(n, m, tokens, grad_out, experts, gates, router_weight, saved_outputs):
    count, width = tokens.shape
    expert_count = router_weight.shape[0]
    layout = (expert_count // n, n, count // 2, width)
    info = jnp.concatenate(
        [experts.T.astype(F32), gates.T.astype(F32), jnp.zeros((4, count), F32)], axis=0
    )
    gathered, weights, logit, router_grad = exchange(
        info, grad_out, tokens, saved_outputs.reshape(layout), expert_count, n, m
    )
    expert_grad, input_grad = finish(weights, gathered, logit, router_weight, layout)
    return (input_grad, router_grad, expert_grad.reshape(saved_outputs.shape))


def solution(mesh):
    spec = P(("dp", "expert"), None)
    return jax.shard_map(
        functools.partial(local, mesh.shape["expert"], mesh.shape["dp"]),
        mesh=mesh,
        in_specs=(spec, spec, spec, spec, P(), spec),
        out_specs=(spec, P(), spec),
        check_vma=False,
    )
```

time: 229 us -> 61 us (0.27)
  waiting for transfers between devices: 145 us -> 0 us
  Pallas kernels: 0 us -> 54.1 us
  local copies, waits for them, and re-layouts: 46.9 us -> 4.43 us
  between operations: 14.2 us -> 0.66 us
  starting transfers between devices: 9.97 us -> 0 us
  other arithmetic: 10.7 us -> 1.41 us
  matrix products: 2.36 us -> 0 us
    psum x1 -> x0, waiting for transfers between devices: 90.1 us -> none  [local(): summed = lax.psum(partial_value, ('dp', 'expert'))]
    all_to_all x2 -> x0, waiting for transfers between devices: 54.6 us -> none  [the longest x1 28.4 us: local(): lax.all_to_all(buffer.reshape(layout), 'expert', split_axis=1, concat_axi...]
    pallas_call x0 -> x2, Pallas kernels: none -> 54.1 us  [the longest x1 46.3 us: exchange(): pl.pallas_call(functools.partial(exchange_kernel, n, m, pieces, scale), n...]
    reshape x6 -> x0, local copies, waits for them, and re-layouts: 20.3 us -> none  [the longest x1 8.69 us: local(): saved_outputs.reshape(layout)]
    all_to_all x2 -> x0, local copies, waits for them, and re-layouts: 14.2 us -> none  [the longest x1 7.13 us: local(): lax.all_to_all(buffer.reshape(layout), 'expert', split_axis=1, concat_axi...]
    all_to_all x2 -> x0, starting transfers between devices: 9.93 us -> none  [the longest x1 4.99 us: local(): lax.all_to_all(saved_outputs.reshape(layout), 'expert', split_axis=1, con...]
    gather x1 -> x0, local copies, waits for them, and re-layouts: 7.96 us -> none  [local(): picked = returned.reshape(-1, width)[target]]
    scatter x1 -> x0, other arithmetic: 6.11 us -> none  [local(): jnp.zeros(saved_outputs.shape, jnp.bfloat16).at[target].set(weighted)]
  transfers between devices with their start and end apart: 3 -> 0, of which waited for: 3 -> 0; matrix products, arithmetic and copies ran while one was open for 22% -> 0% of each run, Pallas kernels for 0% -> 0%
where the time goes in v1:
time: 61 us; the launch traced here: 60.6 us
  Pallas kernels  54.1 us (89%)
  local copies, waits for them, and re-layouts  4.43 us (7%)
  other arithmetic  1.41 us (2%)
  between operations  0.66 us (1%)
    pallas_call x1, Pallas kernels, exchange(): pl.pallas_call(functools.partial(exchange_kernel, n, m, pieces, scale), n...  46.3 us
    pallas_call x1, Pallas kernels, finish(): pl.pallas_call(finish_kernel, name='finish', grid=(n, split), out_shape=(...  7.78 us
    unnamed x9, local copies, waits for them, and re-layouts  4.35 us

profile of v1, /device:TPU:0, one launch (start us, length us, event | category | flops | bytes accessed | tf_op | source)
XLA Modules:
  0.0 60.6 jit_solution(12342549306504709849)
XLA Ops:
  0.6 0.1 pad.2.clone
  0.7 0.7 %convert_bitcast_fusion.1 = f32[2,128]{1,0:T(2,128)S(1)} fusion(s32[128,2]{0,1:T(2,128)} %param.8), kind=kLoop, calls=%fused_computation.2 | loop fusion | flops 256 | bytes 2048 | tf_op jit(solution)/shard_map/convert_element_type | solution.py:404
  1.4 0.7 %convert_bitcast_fusion = f32[2,128]{1,0:T(2,128)S(1)} fusion(bf16[128,2]{0,1:T(2,128)(2,1)} %param.9), kind=kLoop, calls=%fused_computation.1 | loop fusion | flops 256 | bytes 1536 | tf_op jit(solution)/shard_map/convert_element_type | solution.py:404
  2.1 0.1 maximum_maximum_fusion.info_ref
  2.1 0.0 copy-start
  2.1 1.2 %copy-done = bf16[128,4096]{1,0:T(8,128)(2,1)S(1)} copy-done((bf16[128,4096]{1,0:T(8,128)(2,1)S(1)}, bf16[128,4096]{1,0:T(8,128)(2,1)}, u32[]{:S(2)}) %copy-start) | copy-done | bytes 1048600
  3.4 0.0 copy-start.1
  3.4 1.2 %copy-done.1 = bf16[128,4096]{1,0:T(8,128)(2,1)S(1)} copy-done((bf16[128,4096]{1,0:T(8,128)(2,1)S(1)}, bf16[128,4096]{1,0:T(8,128)(2,1)}, u32[]{:S(2)}) %copy-start.1) | copy-done | bytes 1048600
  4.6 46.3 %exchange.1 = (bf16[4,128,4096]{2,1,0:T(8,128)(2,1)}, bf16[4,128,128]{2,1,0:T(8,128)(2,1)S(1)}, bf16[128,8]{1,0:T(8,128)(2,1)S(1)}, f32[8,4096]{1,0:T(8,128)S(1)}) custom-call(f32[8,128]{1,0:T(8,128)S(1)} %maximum_maximum_fusion.info_ref, bf16[128,4096]{1,0:T(8,128)(2,1)S(1)} %copy-done, bf16[128,4096]{1,0:T(8,128)(2,1)S(1)} %copy-done.1, ...), custom_call_target="tpu_custom_call" | custom-call | tf_op jit(solution)/shard_map/exchange/pallas_call | solution.py:324
  50.9 0.0 copy-start.2
  50.9 0.6 %copy-done.2 = bf16[4,128,128]{2,1,0:T(8,128)(2,1)} copy-done((bf16[4,128,128]{2,1,0:T(8,128)(2,1)}, bf16[4,128,128]{2,1,0:T(8,128)(2,1)S(1)}, u32[]{:S(2)}) %copy-start.2) | copy-done | bytes 131096
  51.5 0.0 copy-start.3
  51.5 0.6 copy-done.3
  52.1 7.8 %finish.1 = (bf16[2,4,64,4096]{3,2,1,0:T(8,128)(2,1)}, bf16[128,4096]{1,0:T(8,128)(2,1)}) custom-call(bf16[4,128,128]{2,1,0:T(8,128)(2,1)} %copy-done.2, bf16[4,128,4096]{2,1,0:T(8,128)(2,1)} %get-tuple-element.10.g_ref, bf16[128,8]{1,0:T(8,128)(2,1)} %copy-done.3, bf16[8,4096]{1,0:T(8,128)(2,1)} %rw_ref.1), custom_call_target="tpu_custom_call" | custom-call | tf_op jit(solution)/shard_map/finish/pallas_call | solution.py:378
  59.9 0.7 %copy.10 = f32[8,4096]{1,0:T(8,128)} copy(f32[8,4096]{1,0:T(8,128)S(1)} %get-tuple-element.19) | data formatting | bytes 262144
  (1 shorter events, 0.0 us)
Async XLA Ops:
  2.1 1.2 %copy-start = (bf16[128,4096]{1,0:T(8,128)(2,1)S(1)}, bf16[128,4096]{1,0:T(8,128)(2,1)}, u32[]{:S(2)}) copy-start(bf16[128,4096]{1,0:T(8,128)(2,1)} %g_ref.1) | copy-start | bytes 3145732
  3.4 1.2 %copy-start.1 = (bf16[128,4096]{1,0:T(8,128)(2,1)S(1)}, bf16[128,4096]{1,0:T(8,128)(2,1)}, u32[]{:S(2)}) copy-start(bf16[128,4096]{1,0:T(8,128)(2,1)} %tok_ref.1) | copy-start | bytes 3145732
  50.9 0.7 %copy-start.2 = (bf16[4,128,128]{2,1,0:T(8,128)(2,1)}, bf16[4,128,128]{2,1,0:T(8,128)(2,1)S(1)}, u32[]{:S(2)}) copy-start(bf16[4,128,128]{2,1,0:T(8,128)(2,1)S(1)} %get-tuple-element.9.w_ref) | copy-start | bytes 393220
  51.5 0.6 copy-start.3

commit v2 on v1

--- a/solution.py
+++ b/solution.py
@@ -14,18 +14,18 @@
 
 def exchange_kernel(
     n, m, pieces, scale,
-    info_ref, g_ref, tok_ref, saved_ref,
-    g_out, w_out, logit_out, router_out,
-    slots, saved_v, tok_v, meta_own, meta_in, ret_own, ret_in,
+    experts_hbm, gates_hbm, g_hbm, tok_ref, rw_hbm, saved_ref,
+    eg_hbm, ig_hbm, router_out,
+    eg_out, ig_out, experts_v, gates_v, g_ref, rw_v, info_ref, weights_v, logit_v, slots, saved_v, tok_v, meta_own, meta_in, ret_own, ret_in,
     acc_a, acc_b, part, part_in, dp_in, fin, fin_in,
     g_send, g_recv, meta_send, meta_recv, ret_send, ret_recv,
     part_send, part_recv, dp_send, dp_recv, fin_send, fin_recv,
-    saved_sem, tok_sem, gout_sem,
+    saved_sem, load_sem, eg_sem, ig_sem,
 ):
     held, _, cap, width = saved_ref.shape
     rows = held * cap
     tokens = g_ref.shape[0]
-    experts = logit_out.shape[1]
+    experts = rw_v.shape[0]
     piece = width // pieces
     share = width // n
     pairs = n // 2
@@ -64,13 +64,31 @@
             saved_sem.at[j, h],
         )
 
+    loads = [
+        pltpu.make_async_copy(src, dst, load_sem.at[i])
+        for i, (src, dst) in enumerate(
+            [
+                (experts_hbm, experts_v),
+                (gates_hbm, gates_v),
+                (g_hbm, g_ref),
+                (tok_ref, tok_v),
+                (rw_hbm, rw_v),
+            ]
+        )
+    ]
+    for copy in loads[:3]:
+        copy.start()
     for j in range(n):
         for h in range(held):
             saved_copy(j, h).start()
-    tok_copy = pltpu.make_async_copy(tok_ref, tok_v, tok_sem)
-    tok_copy.start()
-    own_out = pltpu.make_async_copy(g_ref, g_out.at[me], gout_sem.at[0])
-    own_out.start()
+    for copy in loads[3:]:
+        copy.start()
+
+    loads[0].wait()
+    loads[1].wait()
+    info_ref[...] = jnp.concatenate(
+        [experts_v[...].astype(F32), gates_v[...].astype(F32), jnp.zeros((4, tokens), F32)], axis=0
+    )
 
     expert_ids = lax.broadcasted_iota(jnp.int32, (experts, tokens), 0).astype(F32)
     hot = [(info_ref[k : k + 1, :] == expert_ids).astype(F32) for k in range(2)]
@@ -84,6 +102,7 @@
         position = jnp.sum(before * hot[k], axis=0, keepdims=True)
         meta_own[k : k + 1, :] = info_ref[k : k + 1, :] * float(cap) + position
 
+    loads[2].wait()
     pl.semaphore_wait(barrier, n + m - 2)
 
     def g_copy(src, j, c, to):
@@ -134,7 +153,12 @@
     def write_weights(j, meta):
         named = masks(meta)
         weights = jnp.where(named[0], meta[2:3, :], 0.0) + jnp.where(named[1], meta[3:4, :], 0.0)
-        w_out[source(j)] = weights.astype(BF16)
+        weights_v[j] = weights.astype(BF16)
+
+    def spread(j, c, right):
+        block = jnp.dot(weights_v[j], right, preferred_element_type=F32).astype(BF16)
+        for h in range(held):
+            eg_out[h, source(j), :, cols(c)] = block[h * cap : (h + 1) * cap]
 
     def product(j, c, right):
         return lax.dot_general(
@@ -165,9 +189,23 @@
     wait_saved(0)
     write_weights(0, meta_own[...])
     zero = jnp.zeros((rows, tokens), F32)
-    own_total = lax.fori_loop(
-        0, pieces, lambda c, total: total + product(0, c, g_ref[:, cols(c)]), zero
-    )
+
+    def own_step(c, total):
+        spread(0, c, g_ref[:, cols(c)])
+        return total + product(0, c, g_ref[:, cols(c)])
+
+    own_total = lax.fori_loop(0, pieces, own_step, zero)
+    store_copies = []
+
+    def put_out(j):
+        for h in range(held):
+            copy = pltpu.make_async_copy(
+                eg_out.at[h, source(j)], eg_hbm.at[h, source(j)], eg_sem.at[j, h]
+            )
+            copy.start()
+            store_copies.append(copy)
+
+    put_out(0)
     own_first, own_second = picked(meta_own[...], own_total)
 
     for j in range(1, n):
@@ -179,13 +217,7 @@
 
     def take(j, c, acc):
         acc[...] += product(j, c, slots[j - 1, :, cols(c)])
-
-    outs = [own_out]
-
-    def put_out(j):
-        copy = pltpu.make_async_copy(slots.at[j - 1], g_out.at[source(j)], gout_sem.at[j])
-        copy.start()
-        outs.append(copy)
+        spread(j, c, slots[j - 1, :, cols(c)])
 
     acc_a[...] = zero
     wait_saved(1)
@@ -196,8 +228,8 @@
         return carry
 
     lax.fori_loop(0, pieces, partner_step, 0)
+    give_back(1, acc_a[...])
     put_out(1)
-    give_back(1, acc_a[...])
 
     for q in range(1, pairs):
         direct, relayed = 2 * q, 2 * q + 1
@@ -223,11 +255,11 @@
             return carry
 
         lax.fori_loop(1, pieces, step, 0)
-        put_out(direct)
         give_back(direct, acc_a[...])
         relayed_step(pieces - 1)
+        give_back(relayed, acc_b[...])
+        put_out(direct)
         put_out(relayed)
-        give_back(relayed, acc_b[...])
 
     grads = [own_first, own_second]
     for j in range(1, n):
@@ -237,7 +269,7 @@
     blended = gates[0] * grads[0] + gates[1] * grads[1]
     logit = hot[0] * (gates[0] * (grads[0] - blended)) + hot[1] * (gates[1] * (grads[1] - blended))
     logit_low = logit.astype(BF16)
-    tok_copy.wait()
+    loads[3].wait()
     for j in range(n):
         part[j] = jnp.dot(
             logit_low, tok_v[:, j * share : (j + 1) * share], preferred_element_type=F32
@@ -249,7 +281,7 @@
     ]
     for copy in part_copies:
         copy.start()
-    logit_out[...] = logit.T.astype(BF16)
+    logit_v[...] = logit.T.astype(BF16)
     total = part[me]
     for j in range(1, n):
         part_copies[j - 1].wait_recv()
@@ -275,6 +307,18 @@
         return carry
 
     lax.fori_loop(1, m, dp_start, 0)
+    loads[4].wait()
+
+    def input_step(c, carry):
+        ig_out[:, cols(c)] = jnp.dot(
+            logit_v[...], rw_v[:, cols(c)], preferred_element_type=F32
+        ).astype(BF16)
+        return carry
+
+    lax.fori_loop(0, pieces, input_step, 0)
+    ig_copy = pltpu.make_async_copy(ig_out, ig_hbm, ig_sem)
+    ig_copy.start()
+    store_copies.append(ig_copy)
     lax.fori_loop(1, m, dp_wait, 0)
     fin[...] = (
         lax.fori_loop(0, m, lambda i, t: t + dp_in[i], jnp.zeros((experts, share), F32)) * scale
@@ -304,35 +348,44 @@
     lax.fori_loop(1, m, dp_sent, 0)
     for copy in meta_copies + ret_copies + part_copies + fin_copies:
         copy.wait_send()
-    for copy in outs:
+    for copy in store_copies:
         copy.wait()
     for j in range(1, n):
         fin_copies[j - 1].wait_recv()
         router_out[:, lanes(source(j))] = fin_in[j - 1]
 
 
-def exchange(info, grad_out, tokens, saved, experts, n, m):
+def exchange(experts, gates, grad_out, tokens, router_weight, saved, n, m):
     held, _, cap, width = saved.shape
     count = tokens.shape[0]
+    expert_count = router_weight.shape[0]
     rows = held * cap
     pieces = max(1, width // 512)
     share = width // n
     scale = float(m * n * count) ** (-0.5)
     dma = pltpu.SemaphoreType.DMA
     vmem = pl.BlockSpec(memory_space=pltpu.VMEM)
-    anywhere = pl.BlockSpec(memory_space=pl.ANY)
+    hbm = pl.BlockSpec(memory_space=pltpu.HBM)
     return pl.pallas_call(
         functools.partial(exchange_kernel, n, m, pieces, scale),
         name="exchange",
         out_shape=(
-            jax.ShapeDtypeStruct((n, count, width), BF16),
-            jax.ShapeDtypeStruct((n, rows, count), BF16),
-            jax.ShapeDtypeStruct((count, experts), BF16),
-            jax.ShapeDtypeStruct((experts, width), F32),
+            jax.ShapeDtypeStruct((held, n, cap, width), BF16),
+            jax.ShapeDtypeStruct((count, width), BF16),
+            jax.ShapeDtypeStruct((expert_count, width), F32),
         ),
-        in_specs=[vmem, vmem, anywhere, anywhere],
-        out_specs=(anywhere, vmem, vmem, vmem),
+        in_specs=[hbm] * 6,
+        out_specs=(hbm, hbm, vmem),
         scratch_shapes=[
+            pltpu.VMEM((held, n, cap, width), BF16),
+            pltpu.VMEM((count, width), BF16),
+            pltpu.VMEM(experts.shape, experts.dtype),
+            pltpu.VMEM(gates.shape, gates.dtype),
+            pltpu.VMEM((count, width), BF16),
+            pltpu.VMEM((expert_count, width), BF16),
+            pltpu.VMEM((8, count), F32),
+            pltpu.VMEM((n, rows, count), BF16),
+            pltpu.VMEM((count, expert_count), BF16),
             pltpu.VMEM((n - 1, count, width), BF16),
             pltpu.VMEM((n, rows, width), BF16),
             pltpu.VMEM((count, width), BF16),
@@ -342,71 +395,82 @@
             pltpu.VMEM((n - 1, 8, count), F32),
             pltpu.VMEM((rows, count), F32),
             pltpu.VMEM((rows, count), F32),
-            pltpu.VMEM((n, experts, share), F32),
-            pltpu.VMEM((n - 1, experts, share), F32),
-            pltpu.VMEM((m, experts, share), F32),
-            pltpu.VMEM((experts, share), F32),
-            pltpu.VMEM((n - 1, experts, share), F32),
+            pltpu.VMEM((n, expert_count, share), F32),
+            pltpu.VMEM((n - 1, expert_count, share), F32),
+            pltpu.VMEM((m, expert_count, share), F32),
+            pltpu.VMEM((expert_count, share), F32),
+            pltpu.VMEM((n - 1, expert_count, share), F32),
             dma((n - 1, pieces)), dma((n - 1, pieces)),
             dma((n - 1,)), dma((n - 1,)),
             dma((n - 1,)), dma((n - 1,)),
             dma((n - 1,)), dma((n - 1,)),
             dma((m,)), dma((m,)),
             dma((n - 1,)), dma((n - 1,)),
-            dma((n, held)), dma, dma((n,)),
+            dma((n, held)), dma((5,)), dma((n, held)), dma,
         ],
         compiler_params=pltpu.CompilerParams(
-            collective_id=0, has_side_effects=True, vmem_limit_bytes=48 << 20
+            collective_id=0, has_side_effects=True, vmem_limit_bytes=58 << 20
         ),
-    )(info, grad_out, tokens, saved)
-
-
-def finish_kernel(w_ref, g_ref, logit_ref, rw_ref, eg_ref, ig_ref):
-    held, cap = eg_ref.shape[0], eg_ref.shape[2]
-    spread = jnp.dot(w_ref[0], g_ref[0], preferred_element_type=F32).astype(BF16)
-    for h in range(held):
-        eg_ref[h, 0] = spread[h * cap : (h + 1) * cap]
-    ig_ref[...] = jnp.dot(logit_ref[...], rw_ref[...], preferred_element_type=F32).astype(BF16)
-
-
-def finish(weights, gathered, logit, router_weight, layout):
-    held, n, cap, width = layout
-    count, experts = logit.shape
-    rows = held * cap
-    split = 2
-    block = width // split
+    )(experts, gates, grad_out, tokens, router_weight, saved)
+
+
+def store_kernel(
+    eg_ref, ig_ref, router_ref, eg_out, ig_out, router_out, eg_v, ig_v, router_v, in_sem, out_sem
+):
+    held, n = eg_ref.shape[:2]
+    steps = [
+        (src.at[h, s], buf.at[h, s], dst.at[h, s])
+        for src, buf, dst in [(eg_ref, eg_v, eg_out)]
+        for h in range(held)
+        for s in range(n)
+    ]
+    half = ig_ref.shape[0] // 2
+    for k in range(2):
+        part = pl.ds(k * half, half)
+        steps.append((ig_ref.at[part], ig_v.at[part], ig_out.at[part]))
+    steps.append((router_ref, router_v, router_out))
+    loads = [
+        pltpu.make_async_copy(src, buf, in_sem.at[i]) for i, (src, buf, _) in enumerate(steps)
+    ]
+    stores = [
+        pltpu.make_async_copy(buf, dst, out_sem.at[i]) for i, (_, buf, dst) in enumerate(steps)
+    ]
+    for copy in loads:
+        copy.start()
+    for load, put in zip(loads, stores):
+        load.wait()
+        put.start()
+    for copy in stores:
+        copy.wait()
+
+
+def store(expert_grad, input_grad, router_grad):
+    held, n = expert_grad.shape[:2]
+    hbm = pl.BlockSpec(memory_space=pltpu.HBM)
+    arrays = (expert_grad, input_grad, router_grad)
+    count = held * n + 3
     return pl.pallas_call(
-        finish_kernel,
+        store_kernel,
         name="finish",
-        grid=(n, split),
-        out_shape=(
-            jax.ShapeDtypeStruct(layout, BF16),
-            jax.ShapeDtypeStruct((count, width), BF16),
-        ),
-        in_specs=[
-            pl.BlockSpec((1, rows, count), lambda s, c: (s, 0, 0)),
-            pl.BlockSpec((1, count, block), lambda s, c: (s, 0, c)),
-            pl.BlockSpec((count // n, experts), lambda s, c: (s, 0)),
-            pl.BlockSpec((experts, block), lambda s, c: (0, c)),
+        out_shape=tuple(jax.ShapeDtypeStruct(a.shape, a.dtype) for a in arrays),
+        in_specs=[hbm] * 3,
+        out_specs=(hbm,) * 3,
+        scratch_shapes=[
+            *[pltpu.VMEM(a.shape, a.dtype) for a in arrays],
+            pltpu.SemaphoreType.DMA((count,)),
+            pltpu.SemaphoreType.DMA((count,)),
         ],
-        out_specs=(
-            pl.BlockSpec((held, 1, cap, block), lambda s, c: (0, s, 0, c)),
-            pl.BlockSpec((count // n, block), lambda s, c: (s, c)),
-        ),
-    )(weights, gathered, logit, router_weight)
+        compiler_params=pltpu.CompilerParams(vmem_limit_bytes=58 << 20),
+    )(*arrays)
 
 
 def local(n, m, tokens, grad_out, experts, gates, router_weight, saved_outputs):
     count, width = tokens.shape
-    expert_count = router_weight.shape[0]
-    layout = (expert_count // n, n, count // 2, width)
-    info = jnp.concatenate(
-        [experts.T.astype(F32), gates.T.astype(F32), jnp.zeros((4, count), F32)], axis=0
+    layout = (router_weight.shape[0] // n, n, count // 2, width)
+    results = exchange(
+        experts.T, gates.T, grad_out, tokens, router_weight, saved_outputs.reshape(layout), n, m
     )
-    gathered, weights, logit, router_grad = exchange(
-        info, grad_out, tokens, saved_outputs.reshape(layout), expert_count, n, m
-    )
-    expert_grad, input_grad = finish(weights, gathered, logit, router_weight, layout)
+    expert_grad, input_grad, router_grad = store(*results)
     return (input_grad, router_grad, expert_grad.reshape(saved_outputs.shape))
 
 

time: 61 us -> 53.1 us (0.87)
  local copies, waits for them, and re-layouts: 4.43 us -> 0 us
  Pallas kernels: 54.1 us -> 52.3 us
  other arithmetic: 1.41 us -> 0 us
    unnamed x9 -> x0, local copies, waits for them, and re-layouts: 4.35 us -> none
    pallas_call x1, Pallas kernels: 7.78 us -> 4.75 us  [store(): pl.pallas_call(store_kernel, name='finish', out_shape=tuple((jax.ShapeDty...]
    convert_element_type x2 -> x0, other arithmetic: 1.34 us -> none  [the longest x1 0.68 us: local(): experts.T.astype(F32)]
    pallas_call x1, Pallas kernels: 46.3 us -> 47.5 us  [exchange(): pl.pallas_call(functools.partial(exchange_kernel, n, m, pieces, scale), n...]
where the time goes in v2:
time: 53.1 us; the launch traced here: 52.9 us
  Pallas kernels  52.3 us (98%)
  between operations  0.64 us (1%)
    pallas_call x1, Pallas kernels, exchange(): pl.pallas_call(functools.partial(exchange_kernel, n, m, pieces, scale), n...  47.5 us
    pallas_call x1, Pallas kernels, store(): pl.pallas_call(store_kernel, name='finish', out_shape=tuple((jax.ShapeDty...  4.75 us

profile of v2, /device:TPU:0, one launch (start us, length us, event | category | flops | bytes accessed | tf_op | source)
XLA Modules:
  0.0 52.9 jit_solution(14860280131376734662)
XLA Ops:
  0.6 47.5 %exchange.1 = (bf16[2,4,64,4096]{3,2,1,0:T(8,128)(2,1)}, bf16[128,4096]{1,0:T(8,128)(2,1)}, f32[8,4096]{1,0:T(8,128)}) custom-call(s32[2,128]{1,0:T(2,128)} %bitcast.5, bf16[2,128]{1,0:T(2,128)(2,1)} %bitcast.6, bf16[128,4096]{1,0:T(8,128)(2,1)} %g_hbm.1, bf16[128,4096]{1,0:T(8,128)(2,1)} %tok_ref.1, bf16[8,4096]{1,0:T(8,128)(2,1)} %rw_hbm.1, ...), custom_call_target="tpu_custom_call" | custom-call | tf_op jit(solution)/shard_map/exchange/pallas_call | solution.py:369
  48.2 4.7 %finish.1 = (bf16[2,4,64,4096]{3,2,1,0:T(8,128)(2,1)}, bf16[128,4096]{1,0:T(8,128)(2,1)}, f32[8,4096]{1,0:T(8,128)}) custom-call(bf16[2,4,64,4096]{3,2,1,0:T(8,128)(2,1)} %get-tuple-element.9.eg_ref, bf16[128,4096]{1,0:T(8,128)(2,1)} %get-tuple-element.10.ig_ref, f32[8,4096]{1,0:T(8,128)} %get-tuple-element.11.router_ref), custom_call_target="tpu_custom_call" | custom-call | tf_op jit(solution)/shard_map/finish/pallas_call | solution.py:452

commit v3 on v2

--- a/solution.py
+++ b/solution.py
@@ -286,7 +286,7 @@
     for j in range(1, n):
         part_copies[j - 1].wait_recv()
         total = total + part_in[j - 1]
-    dp_in[dp] = total
+    dp_in[dp] = total.astype(BF16)
 
     def dp_copy(slot, i):
         return pltpu.make_async_remote_copy(
@@ -321,7 +321,7 @@
     store_copies.append(ig_copy)
     lax.fori_loop(1, m, dp_wait, 0)
     fin[...] = (
-        lax.fori_loop(0, m, lambda i, t: t + dp_in[i], jnp.zeros((experts, share), F32)) * scale
+        lax.fori_loop(0, m, lambda i, t: t + dp_in[i].astype(F32), jnp.zeros((experts, share), F32)) * scale
     )
     fin_copies = [small_copy(fin, fin_in, fin_send, fin_recv, j, target(j)) for j in range(1, n)]
     for copy in fin_copies:
@@ -397,7 +397,7 @@
             pltpu.VMEM((rows, count), F32),
             pltpu.VMEM((n, expert_count, share), F32),
             pltpu.VMEM((n - 1, expert_count, share), F32),
-            pltpu.VMEM((m, expert_count, share), F32),
+            pltpu.VMEM((m, expert_count, share), BF16),
             pltpu.VMEM((expert_count, share), F32),
             pltpu.VMEM((n - 1, expert_count, share), F32),
             dma((n - 1, pieces)), dma((n - 1, pieces)),

time: 53.1 us -> 51.4 us (0.968)
  Pallas kernels: 52.3 us -> 50.6 us
    pallas_call x1, Pallas kernels: 47.5 us -> 45.8 us  [exchange(): pl.pallas_call(functools.partial(exchange_kernel, n, m, pieces, scale), n...]
where the time goes in v3:
time: 51.4 us; the launch traced here: 51.2 us
  Pallas kernels  50.6 us (98%)
  between operations  0.64 us (1%)
    pallas_call x1, Pallas kernels, exchange(): pl.pallas_call(functools.partial(exchange_kernel, n, m, pieces, scale), n...  45.8 us
    pallas_call x1, Pallas kernels, store(): pl.pallas_call(store_kernel, name='finish', out_shape=tuple((jax.ShapeDty...  4.75 us

profile of v3, /device:TPU:0, one launch (start us, length us, event | category | flops | bytes accessed | tf_op | source)
XLA Modules:
  0.0 51.2 jit_solution(3422439339327833020)
XLA Ops:
  0.6 45.8 %exchange.1 = (bf16[2,4,64,4096]{3,2,1,0:T(8,128)(2,1)}, bf16[128,4096]{1,0:T(8,128)(2,1)}, f32[8,4096]{1,0:T(8,128)}) custom-call(s32[2,128]{1,0:T(2,128)} %bitcast.5, bf16[2,128]{1,0:T(2,128)(2,1)} %bitcast.6, bf16[128,4096]{1,0:T(8,128)(2,1)} %g_hbm.1, bf16[128,4096]{1,0:T(8,128)(2,1)} %tok_ref.1, bf16[8,4096]{1,0:T(8,128)(2,1)} %rw_hbm.1, ...), custom_call_target="tpu_custom_call" | custom-call | tf_op jit(solution)/shard_map/exchange/pallas_call | solution.py:369
  46.5 4.7 %finish.1 = (bf16[2,4,64,4096]{3,2,1,0:T(8,128)(2,1)}, bf16[128,4096]{1,0:T(8,128)(2,1)}, f32[8,4096]{1,0:T(8,128)}) custom-call(bf16[2,4,64,4096]{3,2,1,0:T(8,128)(2,1)} %get-tuple-element.9.eg_ref, bf16[128,4096]{1,0:T(8,128)(2,1)} %get-tuple-element.10.ig_ref, f32[8,4096]{1,0:T(8,128)} %get-tuple-element.11.router_ref), custom_call_target="tpu_custom_call" | custom-call | tf_op jit(solution)/shard_map/finish/pallas_call | solution.py:452
